TPU v7x, 32 devices: a whole 2x2x4 slice. The times are simulated.
32 devices in a mesh: dp: 8 (over z, y), mp: 4 (over x, core).
Axes of the slice: x: 2, y: 2, z: 4, core: 2. Of those that a mesh axis runs over, the one named last changes fastest.
Arguments:
- queries: bfloat16 [4096, 4096], P('dp', 'mp'), may hold values from -6 to 6
- passages: bfloat16 [4096, 4096], P('dp', 'mp'), may hold values from -6 to 6
- labels: int32 [4096], P('dp'), may hold values from 0 to 4095
- projection: bfloat16 [4096, 128], P('mp'), may hold values from -0.09375 to 0.09375
Outputs:
- loss: float32 [4096], P('dp')
- query_embed: bfloat16 [4096, 128], P('dp')
All inputs are finite; a program needn't handle non-finite values.
Results may differ from a plain program's by a relative error of at most 0.0039.
Values may be sent and summed in bfloat16 or wider, within the bound.
A program may use at most 64 MiB of HBM per device.

v0:
```python
import jax
import jax.numpy as jnp
from jax import lax
from jax.sharding import PartitionSpec as P


def merged(part, axis, combine):
    gathered = jax.tree.map(lambda a: lax.all_gather(a, axis), part)

    def take(source):
        return jax.tree.map(lambda a: lax.dynamic_index_in_dim(a, source, 0, False), gathered)

    return lax.fori_loop(
        1, lax.axis_size(axis), lambda source, state: combine(state, take(source)), take(0)
    )


def combine_stats(first, second):
    top = jnp.maximum(first[0], second[0])
    total = first[1] * jnp.exp(first[0] - top) + second[1] * jnp.exp(second[0] - top)
    return (top, total, first[2] + second[2])


def block_columns(count):
    target = 2048
    if count <= target:
        return count
    best = 1
    for option in range(1, target + 1):
        if count % option == 0:
            best = option
    return best


def per_device(queries, passages, labels, projection):
    query_part = jnp.dot(queries, projection, preferred_element_type=jnp.float32)
    passage_part = jnp.dot(passages, projection, preferred_element_type=jnp.float32)
    rows = query_part.shape[0]
    embed = query_part.shape[1]
    query_embed = lax.psum(query_part, "mp").astype(jnp.bfloat16)
    passage_embed = lax.psum_scatter(
        passage_part.astype(jnp.bfloat16), "mp", scatter_dimension=0, tiled=True
    )
    offset = lax.axis_index("mp") * passage_embed.shape[0]
    width = passage_embed.shape[0]
    start_state = (
        jnp.full((rows,), -jnp.inf, jnp.float32),
        jnp.zeros((rows,), jnp.float32),
        jnp.zeros((rows,), jnp.float32),
    )
    piece = lax.all_gather(passage_embed, "dp", axis=0, tiled=True)
    count = piece.shape[0]
    columns_each = block_columns(count)
    blocks = piece.reshape(count // columns_each, columns_each, embed)
    firsts = jnp.arange(blocks.shape[0], dtype=jnp.int32) * columns_each

    def step(state, item):
        block, first = item
        scores = lax.dot_general(
            query_embed, block, (((1,), (1,)), ((), ())), preferred_element_type=jnp.float32
        )
        columns = first + lax.iota(jnp.int32, columns_each)
        passage_ids = columns // width * rows + offset + columns % width
        hit = passage_ids[None, :] == labels[:, None]
        chosen = jnp.sum(jnp.where(hit, scores, 0.0), axis=1)
        block_top = jnp.max(scores, axis=1)
        block_sum = jnp.sum(jnp.exp(scores - block_top[:, None]), axis=1)
        return (combine_stats(state, (block_top, block_sum, chosen)), None)

    result, unused = lax.scan(step, start_state, (blocks, firsts))
    top, total, chosen = merged(result, "mp", combine_stats)
    loss = top + jnp.log(total) - chosen
    return (loss, query_embed)


def solution(mesh):
    return jax.shard_map(
        per_device,
        mesh=mesh,
        in_specs=(P("dp", "mp"), P("dp", "mp"), P("dp"), P("mp", None)),
        out_specs=(P("dp"), P("dp", None)),
        check_vma=False,
    )
```

profile of v0, /device:TPU:0, one launch (start us, length us, event | category | flops | bytes accessed | tf_op | source)
XLA Modules:
  0.0 88.4 jit_solution(6473758463576834238)
XLA Ops:
  7.2 0.0 copy-start
  7.2 0.0 reduce-scatter.2.cloned.1.call-start
  7.2 1.2 %copy-done = bf16[512,1024]{1,0:T(8,128)(2,1)S(1)} copy-done((bf16[512,1024]{1,0:T(8,128)(2,1)S(1)}, bf16[512,1024]{1,0:T(8,128)(2,1)}, u32[]{:S(2)}) %copy-start) | copy-done | bytes 1048600
  8.4 2.0 %convolution_convert_fusion = bf16[512,128]{1,0:T(8,128)(2,1)} fusion(bf16[512,1024]{1,0:T(8,128)(2,1)S(1)} %copy-done, bf16[1024,128]{1,0:T(8,128)(2,1)} %param.9), kind=kOutput, calls=%fused_computation.6 | convolution fusion | flops 134283264 | bytes 1441792 | tf_op jit(solution)/shard_map/dot_general | solution.py:37
  10.4 0.0 reduce-scatter.2.cloned.1.call-update
  10.4 0.0 copy-start.2
  10.5 1.7 %fusion.11 = f32[512,128]{1,0:T(8,128)S(1)} fusion(bf16[512,1024]{1,0:T(8,128)(2,1)} %param.6, bf16[1024,128]{1,0:T(8,128)(2,1)} %param.9), kind=kOutput, calls=%fused_computation.27 | convolution fusion | flops 134217728 | bytes 1572864 | tf_op jit(solution)/shard_map/dot_general | solution.py:36
  12.2 16.3 %all-reduce.1 = bf16[512,128]{1,0:T(8,128)(2,1)S(1)} all-reduce(f32[512,128]{1,0:T(8,128)S(1)} %fusion.11), channel_id=1, replica_groups=mesh['dp'=8,'mp'=4] {'mp'}, use_global_device_ids=true, to_apply=%region_0.0 | all-reduce | flops 65536 | bytes 393216 | tf_op jit(solution)/shard_map/psum | solution.py:40
  28.5 0.0 copy-start.1
  28.5 4.5 %reduce-scatter.2.cloned.1.call-done = bf16[128,128]{1,0:T(8,128)(2,1)} async-done(((bf16[512,128]{1,0:T(8,128)(2,1)}), bf16[128,128]{1,0:T(8,128)(2,1)}) %reduce-scatter.2.cloned.1.call-update) | async-done | bytes 32784 | tf_op jit(solution)/shard_map/reduce_scatter | solution.py:41
  33.0 31.0 %all_gather.19 = bf16[1024,128]{1,0:T(8,128)(2,1)S(1)} all-gather(bf16[128,128]{1,0:T(8,128)(2,1)} %reduce-scatter.2.cloned.1.call-done), channel_id=1, replica_groups=mesh['dp'=8,'mp'=4] {'dp'}, dimensions={0}, use_global_device_ids=true | all-gather | bytes 294912 | tf_op jit(solution)/shard_map/all_gather | solution.py:51
  64.0 0.5 fusion.10
  64.5 0.0 copy-done.2
  64.5 0.7 select_reduce_fusion
  65.2 0.0 copy-done.1
  65.2 5.2 %all-gather.3 = f32[4,1,512]{2,1,0:T(1,128)S(1)} all-gather(f32[1,1,512]{2,1,0:T(1,128)S(1)} %bitcast.40), channel_id=1, replica_groups=mesh['dp'=8,'mp'=4] {'mp'}, dimensions={0}, use_global_device_ids=true | all-gather | bytes 10240 | tf_op jit(solution)/shard_map/all_gather | solution.py:8
  70.4 5.2 %all-gather.4 = f32[4,1,512]{2,1,0:T(1,128)S(1)} all-gather(f32[1,1,512]{2,1,0:T(1,128)S(1)} %bitcast.41), channel_id=3, replica_groups=mesh['dp'=8,'mp'=4] {'mp'}, dimensions={0}, use_global_device_ids=true | all-gather | bytes 10240 | tf_op jit(solution)/shard_map/all_gather | solution.py:8
  75.6 5.2 %all-gather.2 = f32[4,1,512]{2,1,0:T(1,128)S(1)} all-gather(f32[1,1,512]{2,1,0:T(1,128)S(1)} %bitcast.39), channel_id=2, replica_groups=mesh['dp'=8,'mp'=4] {'mp'}, dimensions={0}, use_global_device_ids=true | all-gather | bytes 10240 | tf_op jit(solution)/shard_map/all_gather | solution.py:8
  80.7 0.2 while.12
  81.0 0.6 add_subtract_fusion
  (20 shorter events, 0.2 us)
Async XLA Ops:
  7.2 1.2 %copy-start = (bf16[512,1024]{1,0:T(8,128)(2,1)S(1)}, bf16[512,1024]{1,0:T(8,128)(2,1)}, u32[]{:S(2)}) copy-start(bf16[512,1024]{1,0:T(8,128)(2,1)} %param.7) | copy-start | bytes 3145732
  7.2 25.8 %reduce-scatter.2.cloned.1.call-start = ((), (), s32[]{:S(2)}) async-start(), calls=%async_computation.1 | async-start | bytes 163840 | tf_op jit(solution)/shard_map/reduce_scatter | solution.py:41
  10.4 54.0 %copy-start.2 = (s32[512]{0:T(512)S(1)}, s32[512]{0:T(512)}, u32[]{:S(2)}) copy-start(s32[512]{0:T(512)} %param.8) | copy-start | bytes 6148
  28.5 36.7 %copy-start.1 = (bf16[512,128]{1,0:T(8,128)(2,1)}, bf16[512,128]{1,0:T(8,128)(2,1)S(1)}, u32[]{:S(2)}) copy-start(bf16[512,128]{1,0:T(8,128)(2,1)S(1)} %all-reduce.1) | copy-start | bytes 393220
Sparse Core Ops, SparseCore 0:
  10.6 22.3 reduce-scatter.1
where the time goes:
time: 88.7 us; the launch traced here: 88.4 us
  blocking collectives  62.8 us (71%)
  between operations  14.1 us (16%)
  waiting for transfers between devices  4.51 us (5%)
  matrix products  4.24 us (5%)
  other arithmetic  1.37 us (2%)
  local copies, waits for them, and re-layouts  1.26 us (1%)
    all_gather x1, blocking collectives, per_device(): piece = lax.all_gather(passage_embed, 'dp', axis=0, tiled=True)  31 us
    psum x1, blocking collectives, per_device(): query_embed = lax.psum(query_part, 'mp').astype(jnp.bfloat16)  16.3 us
    all_gather x3, blocking collectives, merged(): gathered = jax.tree.map(lambda a: lax.all_gather(a, axis), part)  15.5 us
    reduce_scatter x1, waiting for transfers between devices, per_device(): lax.psum_scatter(passage_part.astype(jnp.bfloat16), 'mp', scatter_dimensi...  4.5 us
    dot_general x1, matrix products, per_device(): jnp.dot(passages, projection, preferred_element_type=jnp.float32)  2.03 us
  transfers between devices with their start and end apart: 1, of which 1 were waited for; matrix products, arithmetic and copies ran while one was open for 2% of the time, Pallas kernels for 0%

commit v1 on v0

v1 whole, which is shorter than its diff:
```python
import functools

import jax
import jax.numpy as jnp
from jax import lax
from jax.experimental import pallas as pl
from jax.experimental.pallas import tpu as pltpu
from jax.sharding import PartitionSpec as P

MESH = pl.DeviceIdType.MESH


def is_power(count):
    return count & (count - 1) == 0


def flipped(me, step):
    result, bit = me, 1
    while bit <= step:
        if step & bit:
            result = result + bit - 2 * bit * (lax.div(me, bit) % 2)
        bit *= 2
    return result


def peer_to(me, step, count):
    return flipped(me, step) if is_power(count) else lax.rem(me + step, count)


def peer_from(me, step, count):
    return flipped(me, step) if is_power(count) else lax.rem(me - step + count, count)


def kernel(
    sizes,
    queries, passages, labels, projection,
    loss, embed_out,
    weights, q_rows, p_rows, q_send, p_send, q_recv, p_recv, q_all, p_all, stats,
    load_sem, w_sem, out_sem, qs_sem, qr_sem, ps_sem, pr_sem, as_sem, ar_sem, gs_sem, gr_sem, ts_sem, tr_sem,
):
    n_dp, n_mp, n_in = sizes
    n_out = n_dp // n_in
    dp, mp = lax.axis_index("dp"), lax.axis_index("mp")
    outer, inner = lax.div(dp, n_in), lax.rem(dp, n_in)
    rows = queries.shape[0]
    width = rows // n_mp

    order = list(range(n_mp - 1, -1, -1)) if n_mp < 4 else [2, 3] + list(range(4, n_mp)) + [1, 0]

    def chunk(step):
        return pl.ds(pl.multiple_of(peer_to(mp, step, n_mp) * width, width), width)

    weight_copy = pltpu.make_async_copy(projection, weights, w_sem)
    weight_copy.start()
    loads = {}
    for kind, source, held in ((0, passages, p_rows), (1, queries, q_rows)):
        for step in order:
            loads[kind, step] = pltpu.make_async_copy(
                source.at[chunk(step)], held.at[step], load_sem.at[kind, step]
            )
            loads[kind, step].start()

    def out_peer(step):
        return peer_to(outer, step, n_out) * n_in + inner

    def in_peer(step):
        return outer * n_in + peer_to(inner, step, n_in)

    barrier = pltpu.get_barrier_semaphore()
    greeted = 0
    for step in range(1, n_mp):
        pl.semaphore_signal(barrier, device_id={"mp": peer_to(mp, step, n_mp)}, device_id_type=MESH)
        greeted += 1
    for step in range(1, n_in):
        pl.semaphore_signal(barrier, device_id={"dp": in_peer(step)}, device_id_type=MESH)
        greeted += 1
    for step in range(1, n_out):
        pl.semaphore_signal(barrier, device_id={"dp": out_peer(step)}, device_id_type=MESH)
        greeted += 1

    sends = []

    def remote(source, target, send_sem, recv_sem, device):
        copy = pltpu.make_async_remote_copy(
            src_ref=source, dst_ref=target, send_sem=send_sem, recv_sem=recv_sem,
            device_id=device, device_id_type=MESH,
        )
        copy.start()
        sends.append(copy)
        return copy

    weight_copy.wait()
    own = {}
    parts = {}
    first = True
    for kind, held, send, recv, s_sem, r_sem in (
        (0, p_rows, p_send, p_recv, ps_sem, pr_sem),
        (1, q_rows, q_send, q_recv, qs_sem, qr_sem),
    ):
        for step in order:
            loads[kind, step].wait()
            part = jnp.dot(held[step], weights[...], preferred_element_type=jnp.float32)
            if step == 0:
                own[kind] = part
                continue
            send[step] = part.astype(jnp.bfloat16)
            if first:
                pl.semaphore_wait(barrier, greeted)
                first = False
            parts[kind, step] = remote(
                send.at[step], recv.at[step], s_sem.at[step], r_sem.at[step],
                {"mp": peer_to(mp, step, n_mp)},
            )
    if first:
        pl.semaphore_wait(barrier, greeted)

    def added(kind, recv):
        total = own[kind]
        for step in order:
            if step:
                parts[kind, step].wait_recv()
                total = total + recv[step].astype(jnp.float32)
        return total.astype(jnp.bfloat16)

    p_all[0, 0] = added(0, p_recv)
    arrivals = {}
    for step in range(1, n_out):
        arrivals[0, step] = remote(
            p_all.at[0, 0], p_all.at[0, step], gs_sem.at[0, step], gr_sem.at[0, step],
            {"dp": out_peer(step)},
        )

    def relay(out_step):
        for step in range(1, n_in):
            arrivals[step, out_step] = remote(
                p_all.at[0, out_step], p_all.at[step, out_step],
                gs_sem.at[step, out_step], gr_sem.at[step, out_step],
                {"dp": in_peer(step)},
            )

    relay(0)

    mine = pl.ds(pl.multiple_of(mp * width, width), width)
    q_all[mine] = added(1, q_recv)
    embeds = []
    for step in [s for s in order if s]:
        embeds.append(
            remote(
                q_all.at[mine], q_all.at[mine], as_sem.at[step], ar_sem.at[step],
                {"mp": peer_to(mp, step, n_mp)},
            )
        )
    for step in range(1, n_out):
        arrivals[0, step].wait_recv()
        relay(step)
    for copy in embeds:
        copy.wait_recv()
    out_copy = pltpu.make_async_copy(q_all, embed_out, out_sem)
    out_copy.start()

    wanted = labels[...]
    sub = 8
    local_id = lax.broadcasted_iota(jnp.int32, (width, rows), 0)

    def block(in_step, out_step):
        source = peer_from(outer, out_step, n_out) * n_in + peer_from(inner, in_step, n_in)
        scores = lax.dot_general(
            p_all[in_step, out_step], q_all[...], (((1,), (1,)), ((), ())),
            preferred_element_type=jnp.float32,
        )
        hit = local_id == wanted - (source * rows + mp * width)
        chosen = jnp.where(hit, scores, 0.0).reshape(width // sub, sub, rows).sum(axis=0)
        return scores.reshape(width // sub, sub, rows), chosen

    state = None
    for in_step in range(n_in):
        for out_step in range(n_out):
            if in_step:
                arrivals[in_step, out_step].wait_recv()
            scores, chosen = block(in_step, out_step)
            top = scores.max(axis=0)
            if state is None:
                total = jnp.exp(scores - top).sum(axis=0)
            else:
                top = jnp.maximum(top, state[0])
                total = state[1] * jnp.exp(state[0] - top) + jnp.exp(scores - top).sum(axis=0)
                chosen = chosen + state[2]
            state = (top, total, chosen)

    top = state[0].max(axis=0, keepdims=True)
    total = (state[1] * jnp.exp(state[0] - top)).sum(axis=0, keepdims=True)
    own_lse = top + jnp.log(total)
    own_chosen = state[2].sum(axis=0, keepdims=True)
    stats[0, 0:1] = own_lse
    stats[0, 1:2] = own_chosen
    news = []
    for step in [s for s in order if s]:
        news.append(
            remote(
                stats.at[0], stats.at[step], ts_sem.at[step], tr_sem.at[step],
                {"mp": peer_to(mp, step, n_mp)},
            )
        )
    for copy in news:
        copy.wait_recv()
    lses = [own_lse] + [stats[step, 0:1] for step in range(1, n_mp)]
    best = functools.reduce(jnp.maximum, lses)
    spread = sum(jnp.exp(lse - best) for lse in lses)
    picked = own_chosen + sum(stats[step, 1:2] for step in range(1, n_mp))
    loss[...] = best + jnp.log(spread) - picked
    out_copy.wait()
    for copy in sends:
        copy.wait_send()


def per_device(n_dp, n_mp, queries, passages, labels, projection):
    rows, depth = queries.shape
    embed = projection.shape[1]
    width = rows // n_mp
    n_in = 2 if n_dp % 2 == 0 else 1
    n_out = n_dp // n_in
    bf16, f32 = jnp.bfloat16, jnp.float32
    dma = pltpu.SemaphoreType.DMA
    anywhere = pl.BlockSpec(memory_space=pl.ANY)
    vmem = pl.BlockSpec(memory_space=pltpu.VMEM)
    loss, query_embed = pl.pallas_call(
        functools.partial(kernel, (n_dp, n_mp, n_in)),
        out_shape=(
            jax.ShapeDtypeStruct((1, rows), f32),
            jax.ShapeDtypeStruct((rows, embed), bf16),
        ),
        in_specs=[anywhere, anywhere, vmem, anywhere],
        out_specs=(vmem, anywhere),
        scratch_shapes=[
            pltpu.VMEM((depth, embed), bf16),
            pltpu.VMEM((n_mp, width, depth), bf16),
            pltpu.VMEM((n_mp, width, depth), bf16),
            pltpu.VMEM((n_mp, width, embed), bf16),
            pltpu.VMEM((n_mp, width, embed), bf16),
            pltpu.VMEM((n_mp, width, embed), bf16),
            pltpu.VMEM((n_mp, width, embed), bf16),
            pltpu.VMEM((rows, embed), bf16),
            pltpu.VMEM((n_in, n_out, width, embed), bf16),
            pltpu.VMEM((n_mp, 2, rows), f32),
            dma((2, n_mp)),
            dma,
            dma,
            dma((n_mp,)),
            dma((n_mp,)),
            dma((n_mp,)),
            dma((n_mp,)),
            dma((n_mp,)),
            dma((n_mp,)),
            dma((n_in, n_out)),
            dma((n_in, n_out)),
            dma((n_mp,)),
            dma((n_mp,)),
        ],
        compiler_params=pltpu.CompilerParams(collective_id=0, has_side_effects=True),
    )(queries, passages, labels.reshape(1, rows), projection)
    return loss.reshape(rows), query_embed


def solution(mesh):
    return jax.shard_map(
        functools.partial(per_device, mesh.shape["dp"], mesh.shape["mp"]),
        mesh=mesh,
        in_specs=(P("dp", "mp"), P("dp", "mp"), P("dp"), P("mp", None)),
        out_specs=(P("dp"), P("dp", None)),
        check_vma=False,
    )
```

time: 88.7 us -> 25.4 us (0.29)
  blocking collectives: 62.8 us -> 0 us
  Pallas kernels: 0 us -> 21.8 us
  between operations: 14.1 us -> 0.65 us
  waiting for transfers between devices: 4.51 us -> 0 us
  matrix products: 4.24 us -> 0 us
  local copies, waits for them, and re-layouts: 1.26 us -> 2.79 us
  other arithmetic: 1.37 us -> 0 us
    all_gather x4 -> x0, blocking collectives: 46.5 us -> none  [the longest x1 31 us: per_device(): piece = lax.all_gather(passage_embed, 'dp', axis=0, tiled=True)]
    pallas_call x0 -> x1, Pallas kernels: none -> 21.8 us  [per_device(): pl.pallas_call(functools.partial(kernel, (n_dp, n_mp, n_in)), out_shape=(...]
    psum x1 -> x0, blocking collectives: 16.3 us -> none  [per_device(): query_embed = lax.psum(query_part, 'mp').astype(jnp.bfloat16)]
    reduce_scatter x1 -> x0, waiting for transfers between devices: 4.5 us -> none  [per_device(): lax.psum_scatter(passage_part.astype(jnp.bfloat16), 'mp', scatter_dimensi...]
    dot_general x3 -> x0, matrix products: 4.24 us -> none  [the longest x1 2.03 us: per_device(): jnp.dot(passages, projection, preferred_element_type=jnp.float32)]
    unnamed x9 -> x4, local copies, waits for them, and re-layouts: 1.2 us -> 2.79 us
  transfers between devices with their start and end apart: 1 -> 0, of which waited for: 1 -> 0; matrix products, arithmetic and copies ran while one was open for 2% -> 0% of each run, Pallas kernels for 0% -> 0%
where the time goes in v1:
time: 25.4 us; the launch traced here: 25.2 us
  Pallas kernels  21.8 us (86%)
  local copies, waits for them, and re-layouts  2.79 us (11%)
  between operations  0.65 us (3%)
    pallas_call x1, Pallas kernels, per_device(): pl.pallas_call(functools.partial(kernel, (n_dp, n_mp, n_in)), out_shape=(...  21.8 us
    unnamed x4, local copies, waits for them, and re-layouts  2.79 us

profile of v1, /device:TPU:0, one launch (start us, length us, event | category | flops | bytes accessed | tf_op | source)
XLA Modules:
  0.0 25.2 jit_solution(11456539189643502099)
XLA Ops:
  0.6 21.8 %shard_map.59 = (f32[1,512]{1,0:T(1,128)}, bf16[512,128]{1,0:T(8,128)(2,1)}) custom-call(bf16[512,1024]{1,0:T(8,128)(2,1)} %queries.1, bf16[512,1024]{1,0:T(8,128)(2,1)} %passages.1, s32[1,512]{1,0:T(1,128)} %bitcast.3, bf16[1024,128]{1,0:T(8,128)(2,1)} %projection.1), custom_call_target="tpu_custom_call" | custom-call | tf_op jit(solution)/shard_map/pallas_call | solution.py:226
  22.4 0.0 copy-start
  22.4 0.6 %copy-done = f32[1,512]{1,0:T(1,128)S(1)} copy-done((f32[1,512]{1,0:T(1,128)S(1)}, f32[1,512]{1,0:T(1,128)}, u32[]{:S(2)}) %copy-start) | copy-done | bytes 2072
  23.1 0.6 %copy.8 = f32[512]{0:T(512)} copy(f32[512]{0:T(512)S(1)} %bitcast.2) | data formatting | bytes 4096
  23.6 1.6 %copy.9 = bf16[512,128]{1,0:T(8,128)(2,1)} copy(bf16[512,128]{1,0:T(8,128)(2,1)} %get-tuple-element.9) | data formatting | bytes 262144
Async XLA Ops:
  22.4 0.7 %copy-start = (f32[1,512]{1,0:T(1,128)S(1)}, f32[1,512]{1,0:T(1,128)}, u32[]{:S(2)}) copy-start(f32[1,512]{1,0:T(1,128)} %get-tuple-element.4) | copy-start | bytes 6148

commit v2 on v1

--- a/solution.py
+++ b/solution.py
@@ -8,6 +8,7 @@
 from jax.sharding import PartitionSpec as P
 
 MESH = pl.DeviceIdType.MESH
+DIRECT = True
 
 
 def is_power(count):
@@ -34,9 +35,9 @@
 def kernel(
     sizes,
     queries, passages, labels, projection,
-    loss, embed_out,
-    weights, q_rows, p_rows, q_send, p_send, q_recv, p_recv, q_all, p_all, stats,
-    load_sem, w_sem, out_sem, qs_sem, qr_sem, ps_sem, pr_sem, as_sem, ar_sem, gs_sem, gr_sem, ts_sem, tr_sem,
+    stats_out, embed_out,
+    weights, q_rows, p_rows, q_send, p_send, q_recv, p_recv, q_all, p_all, stats, wanted_ref,
+    load_sem, w_sem, label_sem, up_sem, down_sem, qs_sem, qr_sem, ps_sem, pr_sem, as_sem, ar_sem, gs_sem, gr_sem, ts_sem, tr_sem,
 ):
     n_dp, n_mp, n_in = sizes
     n_out = n_dp // n_in
@@ -60,6 +61,9 @@
             )
             loads[kind, step].start()
 
+    label_copy = pltpu.make_async_copy(labels, wanted_ref, label_sem)
+    label_copy.start()
+
     def out_peer(step):
         return peer_to(outer, step, n_out) * n_in + inner
 
@@ -74,9 +78,52 @@
     for step in range(1, n_in):
         pl.semaphore_signal(barrier, device_id={"dp": in_peer(step)}, device_id_type=MESH)
         greeted += 1
-    for step in range(1, n_out):
-        pl.semaphore_signal(barrier, device_id={"dp": out_peer(step)}, device_id_type=MESH)
-        greeted += 1
+    def along(where):
+        return {"dp": where * n_in + inner}
+
+    @pl.when(outer > 0)
+    def _():
+        pl.semaphore_signal(barrier, device_id=along(outer - 1), device_id_type=MESH)
+
+    @pl.when(outer < n_out - 1)
+    def _():
+        pl.semaphore_signal(barrier, device_id=along(outer + 1), device_id_type=MESH)
+
+    greeted = greeted + (outer > 0).astype(jnp.int32) + (outer < n_out - 1).astype(jnp.int32)
+
+    begin = 0 if DIRECT else 1
+    end = n_out - 1 - begin
+
+    def open_line():
+        pl.semaphore_wait(barrier, greeted)
+
+        @pl.when((outer == begin) & (outer < n_out - 1))
+        def _():
+            pl.semaphore_signal(up_sem, device_id=along(outer + 1), device_id_type=MESH)
+
+        @pl.when((outer == end) & (outer > 0))
+        def _():
+            pl.semaphore_signal(down_sem, device_id=along(outer - 1), device_id_type=MESH)
+
+    def pass_on():
+        @pl.when((outer > begin) & (outer < n_out - 1))
+        def _():
+            pl.semaphore_wait(up_sem, 1)
+            pl.semaphore_signal(up_sem, device_id=along(outer + 1), device_id_type=MESH)
+
+        @pl.when((outer < end) & (outer > 0))
+        def _():
+            pl.semaphore_wait(down_sem, 1)
+            pl.semaphore_signal(down_sem, device_id=along(outer - 1), device_id_type=MESH)
+
+    def close_line():
+        @pl.when((outer > begin) & (outer == n_out - 1))
+        def _():
+            pl.semaphore_wait(up_sem, 1)
+
+        @pl.when((outer < end) & (outer == 0))
+        def _():
+            pl.semaphore_wait(down_sem, 1)
 
     sends = []
 
@@ -105,14 +152,15 @@
                 continue
             send[step] = part.astype(jnp.bfloat16)
             if first:
-                pl.semaphore_wait(barrier, greeted)
+                open_line()
                 first = False
             parts[kind, step] = remote(
                 send.at[step], recv.at[step], s_sem.at[step], r_sem.at[step],
                 {"mp": peer_to(mp, step, n_mp)},
             )
     if first:
-        pl.semaphore_wait(barrier, greeted)
+        open_line()
+    pass_on()
 
     def added(kind, recv):
         total = own[kind]
@@ -123,22 +171,27 @@
         return total.astype(jnp.bfloat16)
 
     p_all[0, 0] = added(0, p_recv)
+    close_line()
     arrivals = {}
-    for step in range(1, n_out):
-        arrivals[0, step] = remote(
-            p_all.at[0, 0], p_all.at[0, step], gs_sem.at[0, step], gr_sem.at[0, step],
-            {"dp": out_peer(step)},
+
+    def share(source, in_step, out_step, device):
+        arrivals[in_step, out_step] = remote(
+            source, p_all.at[in_step, out_step], gs_sem.at[in_step, out_step], gr_sem.at[in_step, out_step], device
         )
 
     def relay(out_step):
         for step in range(1, n_in):
-            arrivals[step, out_step] = remote(
-                p_all.at[0, out_step], p_all.at[step, out_step],
-                gs_sem.at[step, out_step], gr_sem.at[step, out_step],
-                {"dp": in_peer(step)},
-            )
-
+            share(p_all.at[0, out_step], step, out_step, {"dp": in_peer(step)})
+
+    out_order = list(range(1, n_out))
     relay(0)
+    for step in out_order:
+        share(p_all.at[0, 0], 0, step, {"dp": out_peer(step)})
+    if DIRECT:
+        for step in out_order:
+            for turn in range(1, n_in):
+                device = peer_to(outer, step, n_out) * n_in + peer_to(inner, turn, n_in)
+                share(p_all.at[0, 0], turn, step, {"dp": device})
 
     mine = pl.ds(pl.multiple_of(mp * width, width), width)
     q_all[mine] = added(1, q_recv)
@@ -150,15 +203,16 @@
                 {"mp": peer_to(mp, step, n_mp)},
             )
         )
-    for step in range(1, n_out):
-        arrivals[0, step].wait_recv()
-        relay(step)
+    if not DIRECT:
+        for step in out_order:
+            arrivals[0, step].wait_recv()
+            relay(step)
     for copy in embeds:
         copy.wait_recv()
-    out_copy = pltpu.make_async_copy(q_all, embed_out, out_sem)
-    out_copy.start()
-
-    wanted = labels[...]
+    embed_out[...] = q_all[...]
+
+    label_copy.wait()
+    wanted = wanted_ref[...]
     sub = 8
     local_id = lax.broadcasted_iota(jnp.int32, (width, rows), 0)
 
@@ -175,7 +229,7 @@
     state = None
     for in_step in range(n_in):
         for out_step in range(n_out):
-            if in_step:
+            if in_step or (out_step and DIRECT):
                 arrivals[in_step, out_step].wait_recv()
             scores, chosen = block(in_step, out_step)
             top = scores.max(axis=0)
@@ -203,14 +257,19 @@
         )
     for copy in news:
         copy.wait_recv()
-    lses = [own_lse] + [stats[step, 0:1] for step in range(1, n_mp)]
+    stats_out[...] = stats[...]
+    for copy in sends:
+        copy.wait_send()
+
+
+def finish(stats, embed, loss, embed_out):
+    n_mp = stats.shape[0]
+    lses = [stats[step, 0:1] for step in range(n_mp)]
     best = functools.reduce(jnp.maximum, lses)
     spread = sum(jnp.exp(lse - best) for lse in lses)
-    picked = own_chosen + sum(stats[step, 1:2] for step in range(1, n_mp))
+    picked = sum(stats[step, 1:2] for step in range(n_mp))
     loss[...] = best + jnp.log(spread) - picked
-    out_copy.wait()
-    for copy in sends:
-        copy.wait_send()
+    embed_out[...] = embed[...]
 
 
 def per_device(n_dp, n_mp, queries, passages, labels, projection):
@@ -223,14 +282,14 @@
     dma = pltpu.SemaphoreType.DMA
     anywhere = pl.BlockSpec(memory_space=pl.ANY)
     vmem = pl.BlockSpec(memory_space=pltpu.VMEM)
-    loss, query_embed = pl.pallas_call(
+    stats, query_embed = pl.pallas_call(
         functools.partial(kernel, (n_dp, n_mp, n_in)),
         out_shape=(
-            jax.ShapeDtypeStruct((1, rows), f32),
-            jax.ShapeDtypeStruct((rows, embed), bf16),
+            pltpu.VMEM((n_mp, 2, rows), f32),
+            pltpu.VMEM((rows, embed), bf16),
         ),
-        in_specs=[anywhere, anywhere, vmem, anywhere],
-        out_specs=(vmem, anywhere),
+        in_specs=[anywhere, anywhere, anywhere, anywhere],
+        out_specs=(vmem, vmem),
         scratch_shapes=[
             pltpu.VMEM((depth, embed), bf16),
             pltpu.VMEM((n_mp, width, depth), bf16),
@@ -242,9 +301,12 @@
             pltpu.VMEM((rows, embed), bf16),
             pltpu.VMEM((n_in, n_out, width, embed), bf16),
             pltpu.VMEM((n_mp, 2, rows), f32),
+            pltpu.VMEM((1, rows), jnp.int32),
             dma((2, n_mp)),
             dma,
             dma,
+            pltpu.SemaphoreType.REGULAR,
+            pltpu.SemaphoreType.REGULAR,
             dma((n_mp,)),
             dma((n_mp,)),
             dma((n_mp,)),
@@ -258,6 +320,16 @@
         ],
         compiler_params=pltpu.CompilerParams(collective_id=0, has_side_effects=True),
     )(queries, passages, labels.reshape(1, rows), projection)
+    loss, query_embed = pl.pallas_call(
+        finish,
+        out_shape=(
+            jax.ShapeDtypeStruct((1, rows), f32),
+            jax.ShapeDtypeStruct((rows, embed), bf16),
+        ),
+        in_specs=[vmem, vmem],
+        out_specs=(vmem, vmem),
+        compiler_params=pltpu.CompilerParams(vmem_limit_bytes=2**21),
+    )(*(pltpu.with_memory_space_constraint(a, pltpu.VMEM) for a in (stats, query_embed)))
     return loss.reshape(rows), query_embed
 
 

time: 25.4 us -> 21.7 us (0.85)
  local copies, waits for them, and re-layouts: 2.79 us -> 0 us
  Pallas kernels: 21.8 us -> 20.9 us
    unnamed x4 -> x0, local copies, waits for them, and re-layouts: 2.79 us -> none
    pallas_call x1, Pallas kernels: 21.8 us -> 20.3 us  [per_device(): pl.pallas_call(functools.partial(kernel, (n_dp, n_mp, n_in)), out_shape=(...]
    pallas_call x0 -> x1, Pallas kernels: none -> 0.67 us  [per_device(): pl.pallas_call(finish, out_shape=(jax.ShapeDtypeStruct((1, rows), f32), j...]
where the time goes in v2:
time: 21.7 us; the launch traced here: 21.6 us
  Pallas kernels  20.9 us (96%)
  between operations  0.64 us (3%)
    pallas_call x1, Pallas kernels, per_device(): pl.pallas_call(functools.partial(kernel, (n_dp, n_mp, n_in)), out_shape=(...  20.3 us
    pallas_call x1, Pallas kernels, per_device(): pl.pallas_call(finish, out_shape=(jax.ShapeDtypeStruct((1, rows), f32), j...  0.67 us

profile of v2, /device:TPU:0, one launch (start us, length us, event | category | flops | bytes accessed | tf_op | source)
XLA Modules:
  0.0 21.6 jit_solution(1019167331499171533)
XLA Ops:
  0.6 20.3 %shard_map.59 = (f32[4,2,512]{2,1,0:T(2,128)S(1)}, bf16[512,128]{1,0:T(8,128)(2,1)S(1)}) custom-call(bf16[512,1024]{1,0:T(8,128)(2,1)} %queries.1, bf16[512,1024]{1,0:T(8,128)(2,1)} %passages.1, s32[1,512]{1,0:T(1,128)} %bitcast.2, bf16[1024,128]{1,0:T(8,128)(2,1)} %projection.1), custom_call_target="tpu_custom_call" | custom-call | tf_op jit(solution)/shard_map/pallas_call | solution.py:285
  20.9 0.7 %shard_map.60 = (f32[1,512]{1,0:T(1,128)}, bf16[512,128]{1,0:T(8,128)(2,1)}) custom-call(f32[4,2,512]{2,1,0:T(2,128)S(1)} %get-tuple-element.6.stats, bf16[512,128]{1,0:T(8,128)(2,1)S(1)} %get-tuple-element.7.embed), custom_call_target="tpu_custom_call" | custom-call | tf_op jit(solution)/shard_map/pallas_call | solution.py:323

commit v3 on v2

--- a/solution.py
+++ b/solution.py
@@ -184,14 +184,14 @@
             share(p_all.at[0, out_step], step, out_step, {"dp": in_peer(step)})
 
     out_order = list(range(1, n_out))
+    relayed = [step for step in out_order if not DIRECT or step < n_out - 1]
     relay(0)
     for step in out_order:
         share(p_all.at[0, 0], 0, step, {"dp": out_peer(step)})
-    if DIRECT:
-        for step in out_order:
-            for turn in range(1, n_in):
-                device = peer_to(outer, step, n_out) * n_in + peer_to(inner, turn, n_in)
-                share(p_all.at[0, 0], turn, step, {"dp": device})
+    for step in [o for o in out_order if o not in relayed]:
+        for turn in range(1, n_in):
+            device = peer_to(outer, step, n_out) * n_in + peer_to(inner, turn, n_in)
+            share(p_all.at[0, 0], turn, step, {"dp": device})
 
     mine = pl.ds(pl.multiple_of(mp * width, width), width)
     q_all[mine] = added(1, q_recv)
@@ -203,10 +203,9 @@
                 {"mp": peer_to(mp, step, n_mp)},
             )
         )
-    if not DIRECT:
-        for step in out_order:
-            arrivals[0, step].wait_recv()
-            relay(step)
+    for step in relayed:
+        arrivals[0, step].wait_recv()
+        relay(step)
     for copy in embeds:
         copy.wait_recv()
     embed_out[...] = q_all[...]
@@ -229,7 +228,7 @@
     state = None
     for in_step in range(n_in):
         for out_step in range(n_out):
-            if in_step or (out_step and DIRECT):
+            if in_step or (out_step and out_step not in relayed):
                 arrivals[in_step, out_step].wait_recv()
             scores, chosen = block(in_step, out_step)
             top = scores.max(axis=0)

time: 21.7 us -> 20.8 us (0.959)
  Pallas kernels: 20.9 us -> 20 us
    pallas_call x1, Pallas kernels: 20.3 us -> 19.3 us  [per_device(): pl.pallas_call(functools.partial(kernel, (n_dp, n_mp, n_in)), out_shape=(...]
where the time goes in v3:
time: 20.8 us; the launch traced here: 20.6 us
  Pallas kernels  20 us (96%)
  between operations  0.64 us (3%)
    pallas_call x1, Pallas kernels, per_device(): pl.pallas_call(functools.partial(kernel, (n_dp, n_mp, n_in)), out_shape=(...  19.3 us
    pallas_call x1, Pallas kernels, per_device(): pl.pallas_call(finish, out_shape=(jax.ShapeDtypeStruct((1, rows), f32), j...  0.67 us

profile of v3, /device:TPU:0, one launch (start us, length us, event | category | flops | bytes accessed | tf_op | source)
XLA Modules:
  0.0 20.6 jit_solution(8246119338443448096)
XLA Ops:
  0.6 19.3 %shard_map.59 = (f32[4,2,512]{2,1,0:T(2,128)S(1)}, bf16[512,128]{1,0:T(8,128)(2,1)S(1)}) custom-call(bf16[512,1024]{1,0:T(8,128)(2,1)} %queries.1, bf16[512,1024]{1,0:T(8,128)(2,1)} %passages.1, s32[1,512]{1,0:T(1,128)} %bitcast.2, bf16[1024,128]{1,0:T(8,128)(2,1)} %projection.1), custom_call_target="tpu_custom_call" | custom-call | tf_op jit(solution)/shard_map/pallas_call | solution.py:284
  20.0 0.7 %shard_map.60 = (f32[1,512]{1,0:T(1,128)}, bf16[512,128]{1,0:T(8,128)(2,1)}) custom-call(f32[4,2,512]{2,1,0:T(2,128)S(1)} %get-tuple-element.6.stats, bf16[512,128]{1,0:T(8,128)(2,1)S(1)} %get-tuple-element.7.embed), custom_call_target="tpu_custom_call" | custom-call | tf_op jit(solution)/shard_map/pallas_call | solution.py:322

commit v4 on v3

--- a/solution.py
+++ b/solution.py
@@ -171,7 +171,6 @@
         return total.astype(jnp.bfloat16)
 
     p_all[0, 0] = added(0, p_recv)
-    close_line()
     arrivals = {}
 
     def share(source, in_step, out_step, device):
@@ -186,7 +185,11 @@
     out_order = list(range(1, n_out))
     relayed = [step for step in out_order if not DIRECT or step < n_out - 1]
     relay(0)
-    for step in out_order:
+    greeted_steps = out_order[:1] if is_power(n_out) else []
+    for step in greeted_steps:
+        share(p_all.at[0, 0], 0, step, {"dp": out_peer(step)})
+    close_line()
+    for step in out_order[len(greeted_steps):]:
         share(p_all.at[0, 0], 0, step, {"dp": out_peer(step)})
     for step in [o for o in out_order if o not in relayed]:
         for turn in range(1, n_in):

time: 20.8 us -> 20.8 us (level)
  no operation moved by 1% of the time
where the time goes in v4:
time: 20.8 us; the launch traced here: 20.6 us
  Pallas kernels  20 us (96%)
  between operations  0.64 us (3%)
    pallas_call x1, Pallas kernels, per_device(): pl.pallas_call(functools.partial(kernel, (n_dp, n_mp, n_in)), out_shape=(...  19.3 us
    pallas_call x1, Pallas kernels, per_device(): pl.pallas_call(finish, out_shape=(jax.ShapeDtypeStruct((1, rows), f32), j...  0.67 us

profile of v4, /device:TPU:0, one launch (start us, length us, event | category | flops | bytes accessed | tf_op | source)
XLA Modules:
  0.0 20.6 jit_solution(12718002001304715941)
XLA Ops:
  0.6 19.3 %shard_map.59 = (f32[4,2,512]{2,1,0:T(2,128)S(1)}, bf16[512,128]{1,0:T(8,128)(2,1)S(1)}) custom-call(bf16[512,1024]{1,0:T(8,128)(2,1)} %queries.1, bf16[512,1024]{1,0:T(8,128)(2,1)} %passages.1, s32[1,512]{1,0:T(1,128)} %bitcast.2, bf16[1024,128]{1,0:T(8,128)(2,1)} %projection.1), custom_call_target="tpu_custom_call" | custom-call | tf_op jit(solution)/shard_map/pallas_call | solution.py:287
  20.0 0.7 %shard_map.60 = (f32[1,512]{1,0:T(1,128)}, bf16[512,128]{1,0:T(8,128)(2,1)}) custom-call(f32[4,2,512]{2,1,0:T(2,128)S(1)} %get-tuple-element.6.stats, bf16[512,128]{1,0:T(8,128)(2,1)S(1)} %get-tuple-element.7.embed), custom_call_target="tpu_custom_call" | custom-call | tf_op jit(solution)/shard_map/pallas_call | solution.py:325
